TPU v7x, 512 devices: a whole 4x8x8 slice. The times are simulated.
512 devices in a mesh: dp: 32 (over y_hi, x, core), mp: 16 (over y_lo, z).
Axes of the slice: x: 4, y: 8 (y_hi: 4, y_lo: 2; y = y_hi * 2 + y_lo), z: 8, core: 2. Of those that a mesh axis runs over, the one named last changes fastest.
Arguments:
- activations: bfloat16 [32, 128, 4096], P('dp', None, 'mp'), may hold values from -6 to 6
- gradients: bfloat16 [32, 128, 11008], P('dp', None, 'mp'), may hold values from -12 to 12, as said below
- basis_in: bfloat16 [4096, 4096], P(None, 'mp'), may hold values from -0.09375 to 0.09375
- basis_out: bfloat16 [11008, 11008], P('mp', 'dp'), may hold values from -0.0546875 to 0.0546875
Outputs:
- eigen_diag: float32 [11008, 4096], P('dp', 'mp')
Inputs may be any that keep to these rules, and one draw needn't show every extreme that they name: `gradients`: gradients are real-valued with varying scales.
All inputs are finite; a program needn't handle non-finite values.
Results may differ from a plain program's by a relative error of at most 0.02.
Values may be sent and summed in bfloat16 or wider, within the bound.
A program may use at most 64 MiB of HBM per device.

v0:
```python
import jax
import jax.numpy as jnp
from jax import lax
from jax.sharding import PartitionSpec as P


def sent_to_all(shard, axis):
    count = lax.axis_size(axis)
    return lax.all_to_all(
        jnp.broadcast_to(shard[None], (count, *shard.shape)), axis, 0, 0, tiled=True
    )


def joined_along(tiles, dim):
    dims = list(tiles.shape[1:])
    dims[dim] *= tiles.shape[0]
    return jnp.moveaxis(tiles, 0, dim).reshape(dims)


def collect(shard, axis, dim):
    tiles = sent_to_all(shard, axis)
    return joined_along(tiles, dim)


def shards(activations, gradients, basis_in, basis_out):
    gathered = lax.all_gather(gradients, "dp", axis=0, tiled=True)
    seq_count = gathered.shape[0]
    seq_tokens = gathered.shape[1]
    flat_rows = gathered.reshape(seq_count * seq_tokens, gathered.shape[2])
    out_width = basis_out.shape[1]
    partial_sum = jnp.dot(flat_rows, basis_out, preferred_element_type=jnp.float32)
    proj_grad = lax.psum(partial_sum.astype(jnp.bfloat16), "mp")
    proj_grad = proj_grad.reshape(seq_count, seq_tokens, out_width)
    whole_acts = collect(activations, "mp", 2)
    local_tokens = whole_acts.shape[0] * whole_acts.shape[1]
    act_rows = whole_acts.reshape(local_tokens, whole_acts.shape[2])
    proj_act = jnp.dot(act_rows, basis_in, preferred_element_type=jnp.float32).astype(jnp.bfloat16)
    proj_act = proj_act.reshape(whole_acts.shape[0], whole_acts.shape[1], basis_in.shape[1])
    every_act = collect(proj_act, "dp", 0)
    seq_grad = jnp.einsum("sti,stj->sij", proj_grad, every_act, preferred_element_type=jnp.float32)
    squares = jnp.sum(seq_grad * seq_grad, axis=0)
    return squares * (1.0 / (seq_count * seq_tokens))


def solution(mesh):
    return jax.shard_map(
        shards,
        mesh=mesh,
        in_specs=(P("dp", None, "mp"), P("dp", None, "mp"), P(None, "mp"), P("mp", "dp")),
        out_specs=P("dp", "mp"),
        check_vma=False,
    )
```

profile of v0, /device:TPU:2, one launch (start us, length us, event | category | flops | bytes accessed | tf_op | source)
XLA Modules:
  0.0 298.8 jit_solution(9737288411021023752)
XLA Ops:
  6.5 0.0 copy-start
  6.5 0.0 all-gather.2.cloned.1.call-start
  6.5 0.7 all-gather.2.cloned.1.call-update
  7.3 0.9 copy.11
  8.2 0.2 broadcast_in_dim.14
  8.4 37.5 %all_to_all.10 = bf16[16,1,128,256]{2,3,1,0:T(8,128)(2,1)S(1)} all-to-all(bf16[16,1,128,256]{2,3,1,0:T(8,128)(2,1)S(1)} %broadcast_in_dim.14), channel_id=1, replica_groups=mesh['dp'=32,'mp'=16] {'mp'}, dimensions={0} | all-to-all | bytes 2097152 | tf_op jit(solution)/shard_map/all_to_all | solution.py:9
  46.0 0.0 copy-done
  46.0 0.6 convolution_convert_fusion
  46.5 0.0 copy-start.1
  46.6 1.6 broadcast_in_dim.15
  48.2 9.5 %all-to-all-start.1 = ((bf16[32,1,128,256]{3,2,1,0:T(8,128)(2,1)}), bf16[32,1,128,256]{3,2,1,0:T(8,128)(2,1)}, u32[]{:S(2)}, u32[]{:S(2)}) async-start(bf16[32,1,128,256]{3,2,1,0:T(8,128)(2,1)} %broadcast_in_dim.15), calls=%async_computation.1 | async-start | bytes 4194304 | tf_op jit(solution)/shard_map/all_to_all | solution.py:9
  57.7 0.0 all-reduce.2.cloned.1.call-start
  57.8 57.5 %all-gather.2.cloned.1.call-done = bf16[32,128,688]{1,2,0:T(8,128)(2,1)} async-done(((bf16[1,128,688]{1,2,0:T(8,128)(2,1)}), bf16[32,128,688]{1,2,0:T(8,128)(2,1)}) %all-gather.2.cloned.1.call-update) | async-done | bytes 5636112 | tf_op jit(solution)/shard_map/all_gather | solution.py:26
  115.3 0.0 copy-done.1
  115.3 5.0 %fusion.7 = bf16[43,32,8,128]{3,2,1,0:T(8,128)(2,1)S(1)} fusion(bf16[688,344]{1,0:T(8,128)(2,1)S(1)} %copy-done.1, bf16[32,128,688]{1,2,0:T(8,128)(2,1)} %all-gather.2.cloned.1.call-done), kind=kOutput, calls=%fused_computation.7 | convolution fusion | flops 1940226048 | bytes 8927488 | tf_op jit(solution)/shard_map/dot_general | solution.py:31
  120.3 2.1 copy.24
  122.4 0.0 all-reduce.2.cloned.1.call-update
  122.4 9.0 %all-to-all-done.1 = bf16[32,1,128,256]{3,2,1,0:T(8,128)(2,1)} async-done(((bf16[32,1,128,256]{3,2,1,0:T(8,128)(2,1)}), bf16[32,1,128,256]{3,2,1,0:T(8,128)(2,1)}, u32[]{:S(2)}, u32[]{:S(2)}) %all-to-all-start.1) | async-done | bytes 2097184 | tf_op jit(solution)/shard_map/all_to_all | solution.py:9
  131.3 155.8 %all-reduce.2.cloned.1.call-done = bf16[32,128,344]{1,2,0:T(8,128)(2,1)} async-done(((bf16[32,128,344]{1,2,0:T(8,128)(2,1)}), bf16[32,128,344]{1,2,0:T(8,128)(2,1)}) %all-reduce.2.cloned.1.call-update) | async-done | bytes 2818064 | tf_op jit(solution)/shard_map/psum | solution.py:32
  287.1 4.1 %multiply_reduce_fusion = f32[344,256]{1,0:T(8,128)S(1)} fusion(bf16[32,128,344]{1,2,0:T(8,128)(2,1)} %all-reduce.2.cloned.1.call-done, bf16[32,1,128,256]{3,2,1,0:T(8,128)(2,1)} %all-to-all-done.1), kind=kOutput, calls=%fused_computation | convolution fusion | flops 726968320 | bytes 5267456 | tf_op jit(solution)/shard_map/sti,stj->sij/dot_general | solution.py:40
  291.2 0.8 broadcast_multiply_fusion
Async XLA Ops:
  6.5 39.4 %copy-start = (bf16[4096,256]{1,0:T(8,128)(2,1)S(1)}, bf16[4096,256]{1,0:T(8,128)(2,1)}, u32[]{:S(2)}) copy-start(bf16[4096,256]{1,0:T(8,128)(2,1)} %param.6) | copy-start | bytes 6291460
  6.5 108.7 %all-gather.2.cloned.1.call-start = ((), (), s32[]{:S(2)}) async-start(), calls=%async_computation.2 | async-start | bytes 5812224 | tf_op jit(solution)/shard_map/all_gather | solution.py:26
  46.5 68.7 %copy-start.1 = (bf16[688,344]{1,0:T(8,128)(2,1)S(1)}, bf16[688,344]{1,0:T(8,128)(2,1)}, u32[]{:S(2)}) copy-start(bf16[688,344]{1,0:T(8,128)(2,1)} %param.7) | copy-start | bytes 1420036
  48.2 83.1 %all-to-all-start.1 = ((bf16[32,1,128,256]{3,2,1,0:T(8,128)(2,1)}), bf16[32,1,128,256]{3,2,1,0:T(8,128)(2,1)}, u32[]{:S(2)}, u32[]{:S(2)}) async-start(bf16[32,1,128,256]{3,2,1,0:T(8,128)(2,1)} %broadcast_in_dim.15), calls=%async_computation.1 | async-start | bytes 4194304 | tf_op jit(solution)/shard_map/all_to_all | solution.py:9
  57.7 229.4 %all-reduce.2.cloned.1.call-start = ((), (), s32[]{:S(2)}) async-start(), calls=%async_computation.3 | async-start | bytes 5636096 | tf_op jit(solution)/shard_map/psum | solution.py:32
Sparse Core Ops, SparseCore 0:
  10.5 104.6 all-gather.1
  122.5 164.5 all-reduce.1
where the time goes:
time: 299 us
  waiting for transfers between devices  223 us (75%)
  blocking collectives  37.5 us (13%)
  between operations  13.5 us (5%)
  matrix products  9.65 us (3%)
  starting transfers between devices  9.55 us (3%)
  local copies, waits for them, and re-layouts  4.9 us (2%)
    psum x1, waiting for transfers between devices, shards(): proj_grad = lax.psum(partial_sum.astype(jnp.bfloat16), 'mp')  156 us
    all_gather x1, waiting for transfers between devices, shards(): gathered = lax.all_gather(gradients, 'dp', axis=0, tiled=True)  57.5 us
    all_to_all x1, blocking collectives, sent_to_all(): lax.all_to_all(jnp.broadcast_to(shard[None], (count, *shard.shape)), axis...  37.5 us
    all_to_all x1, starting transfers between devices, sent_to_all(): lax.all_to_all(jnp.broadcast_to(shard[None], (count, *shard.shape)), axis...  9.5 us
    all_to_all x1, waiting for transfers between devices, sent_to_all(): lax.all_to_all(jnp.broadcast_to(shard[None], (count, *shard.shape)), axis...  8.96 us
  transfers between devices with their start and end apart: 3, of which 3 were waited for; matrix products, arithmetic and copies ran while one was open for 4% of the time, Pallas kernels for 0%

commit v1 on v0

--- a/solution.py
+++ b/solution.py
@@ -23,7 +23,15 @@
 
 
 def shards(activations, gradients, basis_in, basis_out):
-    gathered = lax.all_gather(gradients, "dp", axis=0, tiled=True)
+    gathered = jnp.concatenate(
+        jax.lax.all_to_all(
+            jnp.stack([gradients] * jax.lax.axis_size("dp"), axis=0),
+            axis_name="dp",
+            split_axis=0,
+            concat_axis=0,
+        ),
+        axis=0,
+    )
     seq_count = gathered.shape[0]
     seq_tokens = gathered.shape[1]
     flat_rows = gathered.reshape(seq_count * seq_tokens, gathered.shape[2])

time: 299 us -> 380 us (1.27)
  waiting for transfers between devices: 223 us -> 285 us
  starting transfers between devices: 9.55 us -> 22.6 us
  local copies, waits for them, and re-layouts: 4.9 us -> 12.4 us
    all_to_all x0 -> x1, waiting for transfers between devices: none -> 120 us  [shards(): jax.lax.all_to_all(jnp.stack([gradients] * jax.lax.axis_size('dp'), axis=...]
    all_gather x1 -> x0, waiting for transfers between devices: 57.5 us -> none  [shards(): gathered = lax.all_gather(gradients, 'dp', axis=0, tiled=True)]
    all_to_all x1, waiting for transfers between devices: 8.96 us -> 51.3 us  [sent_to_all(): lax.all_to_all(jnp.broadcast_to(shard[None], (count, *shard.shape)), axis...]
    psum x1, waiting for transfers between devices: 156 us -> 114 us  [shards(): proj_grad = lax.psum(partial_sum.astype(jnp.bfloat16), 'mp')]
    all_to_all x0 -> x1, starting transfers between devices: none -> 9.4 us  [shards(): jax.lax.all_to_all(jnp.stack([gradients] * jax.lax.axis_size('dp'), axis=...]
    all_to_all x0 -> x1, local copies, waits for them, and re-layouts: none -> 4.1 us  [shards(): jax.lax.all_to_all(jnp.stack([gradients] * jax.lax.axis_size('dp'), axis=...]
  transfers between devices with their start and end apart: 3 -> 3, of which waited for: 3 -> 3; matrix products, arithmetic and copies ran while one was open for 4% -> 3% of each run, Pallas kernels for 0% -> 0%
where the time goes in v1:
time: 380 us; the launch traced here: 379 us
  waiting for transfers between devices  285 us (75%)
  blocking collectives  37.5 us (10%)
  starting transfers between devices  22.6 us (6%)
  between operations  13.5 us (4%)
  local copies, waits for them, and re-layouts  12.4 us (3%)
  matrix products  7.91 us (2%)
    all_to_all x1, waiting for transfers between devices, shards(): jax.lax.all_to_all(jnp.stack([gradients] * jax.lax.axis_size('dp'), axis=...  120 us
    psum x1, waiting for transfers between devices, shards(): proj_grad = lax.psum(partial_sum.astype(jnp.bfloat16), 'mp')  114 us
    all_to_all x1, waiting for transfers between devices, sent_to_all(): lax.all_to_all(jnp.broadcast_to(shard[None], (count, *shard.shape)), axis...  51.3 us
    all_to_all x1, blocking collectives, sent_to_all(): lax.all_to_all(jnp.broadcast_to(shard[None], (count, *shard.shape)), axis...  37.5 us
    all_to_all x1, starting transfers between devices, sent_to_all(): lax.all_to_all(jnp.broadcast_to(shard[None], (count, *shard.shape)), axis...  13.1 us
    all_to_all x1, starting transfers between devices, shards(): jax.lax.all_to_all(jnp.stack([gradients] * jax.lax.axis_size('dp'), axis=...  9.4 us
  transfers between devices with their start and end apart: 3, of which 3 were waited for; matrix products, arithmetic and copies ran while one was open for 3% of the time, Pallas kernels for 0%

profile of v1, /device:TPU:2, one launch (start us, length us, event | category | flops | bytes accessed | tf_op | source)
XLA Modules:
  0.0 379.4 jit_solution(6745929031014641979)
XLA Ops:
  6.5 0.0 copy-start
  6.5 0.0 copy-start.1
  6.5 1.1 copy.15
  7.7 0.2 broadcast_in_dim.14
  7.9 37.5 %all_to_all.15 = bf16[16,1,128,256]{2,3,1,0:T(8,128)(2,1)S(1)} all-to-all(bf16[16,1,128,256]{2,3,1,0:T(8,128)(2,1)S(1)} %broadcast_in_dim.14), channel_id=1, replica_groups=mesh['dp'=32,'mp'=16] {'mp'}, dimensions={0} | all-to-all | bytes 2097152 | tf_op jit(solution)/shard_map/all_to_all | solution.py:9
  45.4 0.0 copy-done.1
  45.4 3.2 stack.2
  48.6 9.4 %all-to-all-start = ((bf16[32,1,128,688]{2,3,1,0:T(8,128)(2,1)}), bf16[32,1,128,688]{2,3,1,0:T(8,128)(2,1)}, u32[]{:S(2)}, u32[]{:S(2)}) async-start(bf16[32,1,128,688]{2,3,1,0:T(8,128)(2,1)} %stack.2), calls=%async_computation | async-start | bytes 11272192 | tf_op jit(solution)/shard_map/all_to_all | solution.py:27
  58.0 0.0 copy-done
  58.0 0.6 convolution_convert_fusion
  58.6 119.5 %all-to-all-done = bf16[32,1,128,688]{2,3,1,0:T(8,128)(2,1)} async-done(((bf16[32,1,128,688]{2,3,1,0:T(8,128)(2,1)}), bf16[32,1,128,688]{2,3,1,0:T(8,128)(2,1)}, u32[]{:S(2)}, u32[]{:S(2)}) %all-to-all-start) | async-done | bytes 5636128 | tf_op jit(solution)/shard_map/all_to_all | solution.py:27
  178.2 1.6 broadcast_in_dim.15
  179.8 13.1 %all-to-all-start.2 = ((bf16[32,1,128,256]{3,2,1,0:T(8,128)(2,1)}), bf16[32,1,128,256]{3,2,1,0:T(8,128)(2,1)}, u32[]{:S(2)}, u32[]{:S(2)}) async-start(bf16[32,1,128,256]{3,2,1,0:T(8,128)(2,1)} %broadcast_in_dim.15), calls=%async_computation.2 | async-start | bytes 4194304 | tf_op jit(solution)/shard_map/all_to_all | solution.py:9
  192.9 0.0 copy-start.2
  193.0 0.0 all-reduce.2.cloned.1.call-start
  193.0 4.1 %copy.13 = bf16[32,1,128,688]{2,0,3,1:T(8,128)(2,1)S(1)} copy(bf16[32,1,128,688]{2,3,1,0:T(8,128)(2,1)} %all-to-all-done) | data formatting | bytes 11272192 | tf_op jit(solution)/shard_map/all_to_all | solution.py:27
  197.1 0.0 copy-done.2
  197.1 3.3 fusion.7
  200.4 2.1 copy.28
  202.5 0.0 all-reduce.2.cloned.1.call-update
  202.5 51.3 %all-to-all-done.2 = bf16[32,1,128,256]{3,2,1,0:T(8,128)(2,1)} async-done(((bf16[32,1,128,256]{3,2,1,0:T(8,128)(2,1)}), bf16[32,1,128,256]{3,2,1,0:T(8,128)(2,1)}, u32[]{:S(2)}, u32[]{:S(2)}) %all-to-all-start.2) | async-done | bytes 2097184 | tf_op jit(solution)/shard_map/all_to_all | solution.py:9
  253.8 113.9 %all-reduce.2.cloned.1.call-done = bf16[32,128,344]{1,2,0:T(8,128)(2,1)} async-done(((bf16[32,128,344]{1,2,0:T(8,128)(2,1)}), bf16[32,128,344]{1,2,0:T(8,128)(2,1)}) %all-reduce.2.cloned.1.call-update) | async-done | bytes 2818064 | tf_op jit(solution)/shard_map/psum | solution.py:40
  367.7 4.1 %multiply_reduce_fusion = f32[344,256]{1,0:T(8,128)S(1)} fusion(bf16[32,128,344]{1,2,0:T(8,128)(2,1)} %all-reduce.2.cloned.1.call-done, bf16[32,1,128,256]{3,2,1,0:T(8,128)(2,1)} %all-to-all-done.2), kind=kOutput, calls=%fused_computation | convolution fusion | flops 726968320 | bytes 5267456 | tf_op jit(solution)/shard_map/sti,stj->sij/dot_general | solution.py:48
  371.8 0.8 broadcast_multiply_fusion
Async XLA Ops:
  6.5 51.5 %copy-start = (bf16[4096,256]{1,0:T(8,128)(2,1)S(1)}, bf16[4096,256]{1,0:T(8,128)(2,1)}, u32[]{:S(2)}) copy-start(bf16[4096,256]{1,0:T(8,128)(2,1)} %param.6) | copy-start | bytes 6291460
  6.5 38.9 %copy-start.1 = (bf16[1,128,688]{1,2,0:T(8,128)(2,1)S(1)}, bf16[1,128,688]{1,2,0:T(8,128)(2,1)}, u32[]{:S(2)}) copy-start(bf16[1,128,688]{1,2,0:T(8,128)(2,1)} %param.5) | copy-start | bytes 528388
  48.6 129.5 %all-to-all-start = ((bf16[32,1,128,688]{2,3,1,0:T(8,128)(2,1)}), bf16[32,1,128,688]{2,3,1,0:T(8,128)(2,1)}, u32[]{:S(2)}, u32[]{:S(2)}) async-start(bf16[32,1,128,688]{2,3,1,0:T(8,128)(2,1)} %stack.2), calls=%async_computation | async-start | bytes 11272192 | tf_op jit(solution)/shard_map/all_to_all | solution.py:27
  179.8 74.0 %all-to-all-start.2 = ((bf16[32,1,128,256]{3,2,1,0:T(8,128)(2,1)}), bf16[32,1,128,256]{3,2,1,0:T(8,128)(2,1)}, u32[]{:S(2)}, u32[]{:S(2)}) async-start(bf16[32,1,128,256]{3,2,1,0:T(8,128)(2,1)} %broadcast_in_dim.15), calls=%async_computation.2 | async-start | bytes 4194304 | tf_op jit(solution)/shard_map/all_to_all | solution.py:9
  192.9 4.2 %copy-start.2 = (bf16[688,344]{1,0:T(8,128)(2,1)S(1)}, bf16[688,344]{1,0:T(8,128)(2,1)}, u32[]{:S(2)}) copy-start(bf16[688,344]{1,0:T(8,128)(2,1)} %param.7) | copy-start | bytes 1420036
  193.0 174.8 %all-reduce.2.cloned.1.call-start = ((), (), s32[]{:S(2)}) async-start(), calls=%async_computation.3 | async-start | bytes 5636096 | tf_op jit(solution)/shard_map/psum | solution.py:40
Sparse Core Ops, SparseCore 0:
  202.6 165.0 all-reduce.1
